TPU v7x, 32 devices: a whole 2x2x4 slice. The times are simulated.
32 devices in a mesh: trade: 4 (over z), node: 8 (over y, x, core).
Axes of the slice: x: 2, y: 2, z: 4, core: 2. Of those that a mesh axis runs over, the one named last changes fastest.
Arguments:
- values_in: float32 [1024, 16384], P('trade', 'node'), may hold values from 0 to 1
- prob_up: float32 [16, 16384], P(None, 'node'), may hold values from 0.1 to 0.3
- prob_down: float32 [16, 16384], P(None, 'node'), may hold values from 0.1 to 0.3
- discount: float32 [16, 16384], P(None, 'node'), may hold values from 0.9 to 1
- swap_rate: float32 [16, 16384], P(None, 'node'), may hold values from -3 to 3
- annuity: float32 [16, 16384], P(None, 'node'), may hold values from 0.5 to 2
- state_price: float32 [16384], P('node'), may hold values from 3.0517578e-05 to 0.00012207031
- exercise_step: int32 [1024, 4], P('trade'), may hold values from 0 to 15
- strike_bucket: int32 [1024], P('trade'), may hold values from 0 to 63
- notional_sign: int32 [1024], P('trade'), may hold values from 0 to 1
- strike_table: float32 [64], replicated, may hold values from -0.5 to 0.5
Outputs:
- values_out: float32 [1024, 16384], P(('trade', 'node'))
- prices: float32 [1024], P(('trade', 'node'))
- portfolio: float32 [], replicated
All inputs are finite; a program needn't handle non-finite values.
Results may differ from a plain program's by a relative error of at most 0.0003.
Values sent between devices are 32-bit elements; how exact they have to be, the bound alone decides.
A program may use at most 128 MiB of HBM per device.

v0:
```python
import jax
import jax.numpy as jnp
from jax import lax
from jax.sharding import PartitionSpec as P


def strikes_of(bucket, strike_table):
    levels = lax.broadcasted_iota(jnp.int32, (1, strike_table.shape[0]), 1)
    return jnp.sum(
        jnp.where(
            bucket[:, None] == levels, strike_table[None, :], jnp.zeros((), strike_table.dtype)
        ),
        axis=1,
    )


def roll_once(padded, prob_up, prob_down, discount_row):
    middle = 1.0 - prob_up - prob_down
    return discount_row * (
        prob_up * padded[:, 2:] + middle * padded[:, 1:-1] + prob_down * padded[:, :-2]
    )


def exercise(values, active, strike, signs, swap_row, annuity_row):
    payoff = signs[:, None] * annuity_row[None, :] * (swap_row[None, :] - strike[:, None])
    return jnp.where(active[:, None], jnp.maximum(values, payoff), values)


def stack_lattice(prob_up, prob_down, discount, swap_rate, annuity, state_price, first_step):
    span = prob_up.shape[0] - first_step
    spread_price = jnp.broadcast_to(state_price[None, :], (span, state_price.shape[0]))
    return jnp.stack([prob_up, prob_down, discount, swap_rate, annuity, spread_price])


def to_trade_rows(values):
    node_count = lax.axis_size("node")
    node_dev = values.shape[1]
    row_count = values.shape[0] // node_count
    blocks = values.reshape(node_count, row_count, node_dev)
    moved = lax.all_to_all(blocks, "node", split_axis=0, concat_axis=2, tiled=True)
    return moved.reshape(row_count, node_dev * node_count)


def roll_back(values, lattice, exercise_step, strike, signs, split_step, step_count):
    row_count = values.shape[0]
    first_row = lax.axis_index("node") * row_count
    my_dates = lax.dynamic_slice_in_dim(exercise_step, first_row, row_count, 0)
    my_strike = lax.dynamic_slice_in_dim(strike, first_row, row_count, 0)
    my_signs = lax.dynamic_slice_in_dim(signs, first_row, row_count, 0)
    for step in range(split_step, step_count):
        local_step = step - split_step
        padded = jnp.pad(values, ((0, 0), (1, 1)))
        values = roll_once(
            padded, lattice[0, local_step], lattice[1, local_step], lattice[2, local_step]
        )
        active = jnp.any(my_dates == step, axis=1)
        values = exercise(
            values, active, my_strike, my_signs, lattice[3, local_step], lattice[4, local_step]
        )
    prices = jnp.sum(values * lattice[5, 0][None, :], axis=1)
    return (values, prices)


def local(
    values_in,
    prob_up,
    prob_down,
    discount,
    swap_rate,
    annuity,
    state_price,
    exercise_step,
    strike_bucket,
    notional_sign,
    strike_table,
):
    step_count = prob_up.shape[0]
    strike = strikes_of(strike_bucket, strike_table)
    signs = (2 * notional_sign - 1).astype(jnp.float32)
    values = to_trade_rows(values_in)
    local_lattice = stack_lattice(prob_up, prob_down, discount, swap_rate, annuity, state_price, 0)
    lattice = lax.all_gather(local_lattice, "node", axis=2, tiled=True)
    values, prices = roll_back(values, lattice, exercise_step, strike, signs, 0, step_count)
    portfolio = lax.psum(jnp.sum(prices), ("trade", "node")) / values_in.shape[0]
    return (values, prices, portfolio)


def solution(mesh):
    in_specs = (
        P("trade", "node"),
        P(None, "node"),
        P(None, "node"),
        P(None, "node"),
        P(None, "node"),
        P(None, "node"),
        P("node"),
        P("trade", None),
        P("trade"),
        P("trade"),
        P(),
    )
    out_specs = (P(("trade", "node"), None), P(("trade", "node")), P())
    return jax.shard_map(local, mesh=mesh, in_specs=in_specs, out_specs=out_specs, check_vma=False)
```

profile of v0, /device:TPU:0, one launch (start us, length us, event | category | flops | bytes accessed | tf_op | source)
XLA Modules:
  0.0 175.1 jit_solution(9109322315187114257)
XLA Ops:
  7.2 0.9 bitcast_dynamic-update-slice_fusion.4
  8.1 0.9 bitcast_dynamic-update-slice_fusion.3
  9.0 0.9 bitcast_dynamic-update-slice_fusion.2
  10.0 0.9 bitcast_dynamic-update-slice_fusion.1
  10.9 0.9 bitcast_dynamic-update-slice_fusion
  13.5 5.3 %all-to-all-start = ((f32[8,32,2048]{2,1,0:T(8,128)}), f32[8,32,2048]{2,1,0:T(8,128)S(1)}, u32[]{:S(2)}, u32[]{:S(2)}) async-start(f32[8,32,2048]{2,1,0:T(8,128)} %bitcast.102), calls=%async_computation | async-start | bytes 4194304 | tf_op jit(solution)/shard_map/all_to_all | solution.py:40
  19.2 34.6 %all-to-all-done = f32[8,32,2048]{2,1,0:T(8,128)S(1)} async-done(((f32[8,32,2048]{2,1,0:T(8,128)}), f32[8,32,2048]{2,1,0:T(8,128)S(1)}, u32[]{:S(2)}, u32[]{:S(2)}) %all-to-all-start) | async-done | bytes 2097184 | tf_op jit(solution)/shard_map/all_to_all | solution.py:40
  53.8 1.3 copy-done
  55.1 2.2 %copy.17 = f32[4,8,8,2048]{3,1,2,0:T(8,128)S(1)} copy(f32[4,8,8,2048]{3,1,0,2:T(8,128)} %bitcast.101) | data formatting | bytes 4194304
  57.3 19.5 %all-gather.2.cloned.1.call-done = f32[6,16,16384]{2,1,0:T(8,128)} async-done(((f32[6,16,2048]{2,1,0:T(8,128)}), f32[6,16,16384]{2,1,0:T(8,128)}) %all-gather.2.cloned.1.call-update) | async-done | bytes 6291472 | tf_op jit(solution)/shard_map/all_gather | solution.py:82
  76.8 5.8 %fusion.2 = (f32[1,1,16384]{2,1,0:T(1,128)S(1)}, f32[1,1,16384]{2,1,0:T(1,128)S(1)}, f32[1,1,16384]{2,1,0:T(1,128)S(1)}, f32[1,1,16384]{2,1,0:T(1,128)S(1)}, f32...) fusion(f32[6,16,16384]{2,1,0:T(8,128)} %all-gather.2.cloned.1.c, ...), kind=kLoop, calls=%fused_computation.62 | loop fusion | bytes 2490368 | tf_op jit(solution)/shard_map/slice | solution.py:54
  82.7 5.7 %fusion.3 = (f32[1,1,16384]{2,1,0:T(1,128)S(1)}, f32[1,1,16384]{2,1,0:T(1,128)S(1)}, f32[1,1,16384]{2,1,0:T(1,128)S(1)}, f32[1,1,16384]{2,1,0:T(1,128)S(1)}, f32...) fusion(f32[6,16,16384]{2,1,0:T(8,128)} %all-gather.2.cloned.1.c, ...), kind=kLoop, calls=%fused_computation.63 | loop fusion | bytes 2490368 | tf_op jit(solution)/shard_map/slice | solution.py:54
  88.4 5.5 %fusion.1 = (f32[1,1,16384]{2,1,0:T(1,128)S(1)}, f32[1,1,16384]{2,1,0:T(1,128)S(1)}, f32[1,1,16384]{2,1,0:T(1,128)S(1)}, f32[1,1,16384]{2,1,0:T(1,128)S(1)}, f32...) fusion(f32[6,16,16384]{2,1,0:T(8,128)} %all-gather.2.cloned.1.c, ...), kind=kLoop, calls=%fused_computation.61 | loop fusion | bytes 2490368 | tf_op jit(solution)/shard_map/slice | solution.py:54
  94.1 6.1 %fusion = (f32[1,1,16384]{2,1,0:T(1,128)S(1)}, f32[1,1,16384]{2,1,0:T(1,128)S(1)}, f32[1,1,16384]{2,1,0:T(1,128)S(1)}, f32[1,1,16384]{2,1,0:T(1,128)S(1)}, f32[1...) fusion(f32[6,16,16384]{2,1,0:T(8,128)} %all-gather.2.cloned.1.c, ...), kind=kLoop, calls=%fused_computation.60 | loop fusion | bytes 2490368 | tf_op jit(solution)/shard_map/slice | solution.py:54
  100.2 2.1 %fusion.4 = (f32[1,1,16384]{2,1,0:T(1,128)S(1)}, f32[1,1,16384]{2,1,0:T(1,128)S(1)}, f32[1,1,16384]{2,1,0:T(1,128)S(1)}, f32[1,1,16384]{2,1,0:T(1,128)S(1)}, f32[1,1,16384]{2,1,0:T(1,128)S(1)}) fusion(f32[6,16,16384]{2,1,0:T(8,128)} %all-gather.2.cloned.1.call-done), kind=kLoop, calls=%fused_computation.64 | loop fusion | bytes 655360 | tf_op jit(solution)/shard_map/slice | solution.py:54
  102.4 1.4 maximum_select_fusion.15
  103.8 1.4 maximum_select_fusion.14
  105.2 1.4 maximum_select_fusion.13
  106.6 1.4 maximum_select_fusion.12
  107.9 1.6 maximum_select_fusion.11
  109.5 1.4 maximum_select_fusion.10
  110.9 1.4 maximum_select_fusion.9
  112.3 1.4 maximum_select_fusion.8
  113.7 1.4 maximum_select_fusion.7
  115.1 1.4 maximum_select_fusion.6
  116.5 1.4 maximum_select_fusion.5
  117.9 1.4 maximum_select_fusion.4
  119.3 1.4 maximum_select_fusion.3
  120.6 1.6 maximum_select_fusion.2
  122.2 1.4 maximum_select_fusion.1
  123.6 3.4 %multiply_reduce_fusion = (f32[]{:T(128)}, f32[32]{0:T(128)}, f32[32,16384]{1,0:T(8,128)}) fusion(f32[16384]{0:T(1024)S(1)} %bitcast.169, f32[32]{0:T(128)S(1)} %dynamic_slice.11, f32[16384]{0:T(1024)S(1)} %bitcast.170, f32[16384]{0:T(1024)S(1)} %bitcast.171, f32[32]{0:T(128)S(1)} %dynamic_slice.10, f32[16384]{0:T(1024)S(1)} %bitcast.108, ...), kind=kLoop, calls=%fused_computation.16 | loop fusion | flops 7339999 | bytes 4653476 | tf_op jit(solution)/shard_map/reduce_sum | solution.py:84
  127.0 39.5 %psum.7 = f32[]{:T(128)} all-reduce(f32[]{:T(128)} %get-tuple-element.3), channel_id=1, replica_groups=mesh['trade'=4,'node'=8] {'trade','node'}, use_global_device_ids=true, to_apply=%region_19.20 | all-reduce | flops 1 | bytes 8 | tf_op jit(solution)/shard_map/psum | solution.py:84
  (35 shorter events, 2.2 us)
Async XLA Ops:
  7.2 69.7 %all-gather.2.cloned.1.call-start = ((), (), s32[]{:S(2)}) async-start(), calls=%async_computation.1 | async-start | bytes 7077888 | tf_op jit(solution)/shard_map/all_gather | solution.py:82
  12.5 0.9 copy-start.1
  13.4 5.4 %copy-start.2 = (s32[256]{0:T(256)S(1)}, s32[256]{0:T(256)}, u32[]{:S(2)}) copy-start(s32[256]{0:T(256)} %param.20) | copy-start | bytes 3076
  13.4 5.5 %copy-start.3 = (s32[256]{0:T(256)S(1)}, s32[256]{0:T(256)}, u32[]{:S(2)}) copy-start(s32[256]{0:T(256)} %param.19) | copy-start | bytes 3076
  13.5 5.5 %copy-start.5 = (f32[64]{0:T(128)S(1)}, f32[64]{0:T(128)}, u32[]{:S(2)}) copy-start(f32[64]{0:T(128)} %param.21) | copy-start | bytes 772
  13.5 5.6 %copy-start.4 = (s32[256,4]{0,1:T(4,128)S(1)}, s32[256,4]{0,1:T(4,128)}, u32[]{:S(2)}) copy-start(s32[256,4]{0,1:T(4,128)} %param.18) | copy-start | bytes 12292
  13.5 40.3 %all-to-all-start = ((f32[8,32,2048]{2,1,0:T(8,128)}), f32[8,32,2048]{2,1,0:T(8,128)S(1)}, u32[]{:S(2)}, u32[]{:S(2)}) async-start(f32[8,32,2048]{2,1,0:T(8,128)} %bitcast.102), calls=%async_computation | async-start | bytes 4194304 | tf_op jit(solution)/shard_map/all_to_all | solution.py:40
  53.8 1.3 copy-start
Sparse Core Ops, SparseCore 0:
  13.6 63.2 all-gather.1
where the time goes:
time: 176 us; the launch traced here: 175 us
  waiting for transfers between devices  54.1 us (31%)
  blocking collectives  39.5 us (22%)
  local copies, waits for them, and re-layouts  35.1 us (20%)
  other arithmetic  24.9 us (14%)
  between operations  16.2 us (9%)
  starting transfers between devices  5.38 us (3%)
    psum x1, blocking collectives, local(): lax.psum(jnp.sum(prices), ('trade', 'node')) / values_in.shape[0]  39.5 us
    all_to_all x1, waiting for transfers between devices, to_trade_rows(): lax.all_to_all(blocks, 'node', split_axis=0, concat_axis=2, tiled=True)  34.6 us
    select_n x15, other arithmetic, exercise(): return jnp.where(active[:, None], jnp.maximum(values, payoff), values)  21.1 us
    all_gather x1, waiting for transfers between devices, local(): lattice = lax.all_gather(local_lattice, 'node', axis=2, tiled=True)  19.5 us
    slice x3, local copies, waits for them, and re-layouts, roll_back(): lattice[2, local_step]  14 us
    slice x2, local copies, waits for them, and re-layouts, roll_back(): lattice[0, local_step]  11.2 us
    unnamed x18, local copies, waits for them, and re-layouts  9.01 us
    all_to_all x1, starting transfers between devices, to_trade_rows(): lax.all_to_all(blocks, 'node', split_axis=0, concat_axis=2, tiled=True)  5.34 us
  transfers between devices with their start and end apart: 2, of which 2 were waited for; matrix products, arithmetic and copies ran while one was open for 1% of the time, Pallas kernels for 0%

commit v1 on v0

--- a/solution.py
+++ b/solution.py
@@ -79,7 +79,7 @@
     signs = (2 * notional_sign - 1).astype(jnp.float32)
     values = to_trade_rows(values_in)
     local_lattice = stack_lattice(prob_up, prob_down, discount, swap_rate, annuity, state_price, 0)
-    lattice = lax.all_gather(local_lattice, "node", axis=2, tiled=True)
+    lattice = jnp.concatenate(lax.all_gather(local_lattice, "node"), axis=2)
     values, prices = roll_back(values, lattice, exercise_step, strike, signs, 0, step_count)
     portfolio = lax.psum(jnp.sum(prices), ("trade", "node")) / values_in.shape[0]
     return (values, prices, portfolio)

time: 176 us -> 192 us (1.091)
  local copies, waits for them, and re-layouts: 35.1 us -> 51.4 us
    all_gather x0 -> x1, local copies, waits for them, and re-layouts: none -> 9.14 us  [local(): lattice = jnp.concatenate(lax.all_gather(local_lattice, 'node'), axis=2)]
    reshape x0 -> x1, local copies, waits for them, and re-layouts: none -> 7.18 us  [local(): lattice = jnp.concatenate(lax.all_gather(local_lattice, 'node'), axis=2)]
where the time goes in v1:
time: 192 us
  waiting for transfers between devices  54.1 us (28%)
  local copies, waits for them, and re-layouts  51.4 us (27%)
  blocking collectives  39.5 us (21%)
  other arithmetic  25 us (13%)
  between operations  16.2 us (8%)
  starting transfers between devices  5.38 us (3%)
    psum x1, blocking collectives, local(): lax.psum(jnp.sum(prices), ('trade', 'node')) / values_in.shape[0]  39.5 us
    all_to_all x1, waiting for transfers between devices, to_trade_rows(): lax.all_to_all(blocks, 'node', split_axis=0, concat_axis=2, tiled=True)  34.6 us
    select_n x15, other arithmetic, exercise(): return jnp.where(active[:, None], jnp.maximum(values, payoff), values)  21.2 us
    all_gather x1, waiting for transfers between devices, local(): lattice = jnp.concatenate(lax.all_gather(local_lattice, 'node'), axis=2)  19.5 us
    slice x3, local copies, waits for them, and re-layouts, roll_back(): lattice[2, local_step]  14 us
    slice x2, local copies, waits for them, and re-layouts, roll_back(): lattice[0, local_step]  11.2 us
    all_gather x1, local copies, waits for them, and re-layouts, local(): lattice = jnp.concatenate(lax.all_gather(local_lattice, 'node'), axis=2)  9.14 us
    unnamed x18, local copies, waits for them, and re-layouts  9.01 us
  transfers between devices with their start and end apart: 2, of which 2 were waited for; matrix products, arithmetic and copies ran while one was open for 1% of the time, Pallas kernels for 0%

profile of v1, /device:TPU:0, one launch (start us, length us, event | category | flops | bytes accessed | tf_op | source)
XLA Modules:
  0.0 191.5 jit_solution(5548511773800435310)
XLA Ops:
  8.1 0.9 bitcast_dynamic-update-slice_fusion.3
  9.0 0.9 bitcast_dynamic-update-slice_fusion.2
  10.9 0.9 bitcast_dynamic-update-slice_fusion
  13.5 5.3 %all-to-all-start = ((f32[8,32,2048]{2,1,0:T(8,128)}), f32[8,32,2048]{2,1,0:T(8,128)S(1)}, u32[]{:S(2)}, u32[]{:S(2)}) async-start(f32[8,32,2048]{2,1,0:T(8,128)} %bitcast.110), calls=%async_computation | async-start | bytes 4194304 | tf_op jit(solution)/shard_map/all_to_all | solution.py:40
  19.2 34.6 %all-to-all-done = f32[8,32,2048]{2,1,0:T(8,128)S(1)} async-done(((f32[8,32,2048]{2,1,0:T(8,128)}), f32[8,32,2048]{2,1,0:T(8,128)S(1)}, u32[]{:S(2)}, u32[]{:S(2)}) %all-to-all-start) | async-done | bytes 2097184 | tf_op jit(solution)/shard_map/all_to_all | solution.py:40
  53.8 1.3 copy-done
  55.1 2.2 %copy.22 = f32[4,8,8,2048]{3,1,2,0:T(8,128)S(1)} copy(f32[4,8,8,2048]{3,1,0,2:T(8,128)} %bitcast.108) | data formatting | bytes 4194304
  57.3 19.5 %all-gather.3.cloned.1.call-done = f32[48,16,2048]{2,1,0:T(8,128)} async-done(((f32[6,16,2048]{2,1,0:T(8,128)}), f32[48,16,2048]{2,1,0:T(8,128)}) %all-gather.3.cloned.1.call-update) | async-done | bytes 6291472 | tf_op jit(solution)/shard_map/all_gather | solution.py:82
  76.8 9.1 %copy.25 = f32[8,6,16,2048]{3,0,2,1:T(8,128)} copy(f32[8,6,16,2048]{3,2,1,0:T(8,128)} %bitcast.109) | data formatting | bytes 12582912 | tf_op jit(solution)/shard_map/all_gather | solution.py:82
  86.0 7.2 %reshape.281 = f32[6,16,16384]{2,1,0:T(8,128)} reshape(f32[6,16,8,2048]{3,2,1,0:T(8,128)} %bitcast.106) | data formatting | bytes 12582912 | tf_op jit(solution)/shard_map/reshape | solution.py:82
  93.1 5.8 %fusion.2 = (f32[1,1,16384]{2,1,0:T(1,128)S(1)}, f32[1,1,16384]{2,1,0:T(1,128)S(1)}, f32[1,1,16384]{2,1,0:T(1,128)S(1)}, f32[1,1,16384]{2,1,0:T(1,128)S(1)}, f32...) fusion(f32[6,16,16384]{2,1,0:T(8,128)} %reshape.281), kind=kLoop, calls=%fused_computation.63 | loop fusion | bytes 2490368 | tf_op jit(solution)/shard_map/slice | solution.py:54
  98.9 5.7 %fusion.3 = (f32[1,1,16384]{2,1,0:T(1,128)S(1)}, f32[1,1,16384]{2,1,0:T(1,128)S(1)}, f32[1,1,16384]{2,1,0:T(1,128)S(1)}, f32[1,1,16384]{2,1,0:T(1,128)S(1)}, f32...) fusion(f32[6,16,16384]{2,1,0:T(8,128)} %reshape.281), kind=kLoop, calls=%fused_computation.64 | loop fusion | bytes 2490368 | tf_op jit(solution)/shard_map/slice | solution.py:54
  104.6 5.5 %fusion.1 = (f32[1,1,16384]{2,1,0:T(1,128)S(1)}, f32[1,1,16384]{2,1,0:T(1,128)S(1)}, f32[1,1,16384]{2,1,0:T(1,128)S(1)}, f32[1,1,16384]{2,1,0:T(1,128)S(1)}, f32...) fusion(f32[6,16,16384]{2,1,0:T(8,128)} %reshape.281), kind=kLoop, calls=%fused_computation.62 | loop fusion | bytes 2490368 | tf_op jit(solution)/shard_map/slice | solution.py:54
  110.2 6.1 %fusion = (f32[1,1,16384]{2,1,0:T(1,128)S(1)}, f32[1,1,16384]{2,1,0:T(1,128)S(1)}, f32[1,1,16384]{2,1,0:T(1,128)S(1)}, f32[1,1,16384]{2,1,0:T(1,128)S(1)}, f32[1...) fusion(f32[6,16,16384]{2,1,0:T(8,128)} %reshape.281), kind=kLoop, calls=%fused_computation.61 | loop fusion | bytes 2490368 | tf_op jit(solution)/shard_map/slice | solution.py:54
  116.3 2.1 %fusion.4 = (f32[1,1,16384]{2,1,0:T(1,128)S(1)}, f32[1,1,16384]{2,1,0:T(1,128)S(1)}, f32[1,1,16384]{2,1,0:T(1,128)S(1)}, f32[1,1,16384]{2,1,0:T(1,128)S(1)}, f32[1,1,16384]{2,1,0:T(1,128)S(1)}) fusion(f32[6,16,16384]{2,1,0:T(8,128)} %reshape.281), kind=kLoop, calls=%fused_computation.65 | loop fusion | bytes 655360 | tf_op jit(solution)/shard_map/slice | solution.py:54
  118.7 1.4 maximum_select_fusion.15
  120.1 1.4 maximum_select_fusion.14
  121.5 1.4 maximum_select_fusion.13
  122.9 1.4 maximum_select_fusion.12
  124.3 1.4 maximum_select_fusion.11
  125.7 1.6 maximum_select_fusion.10
  127.3 1.4 maximum_select_fusion.9
  128.6 1.4 maximum_select_fusion.8
  130.0 1.4 maximum_select_fusion.7
  131.4 1.4 maximum_select_fusion.6
  132.8 1.4 maximum_select_fusion.5
  134.2 1.4 maximum_select_fusion.4
  135.6 1.4 maximum_select_fusion.3
  137.0 1.4 maximum_select_fusion.2
  138.4 1.6 maximum_select_fusion.1
  140.0 3.4 %multiply_reduce_fusion = (f32[]{:T(128)}, f32[32]{0:T(128)}, f32[32,16384]{1,0:T(8,128)}) fusion(f32[16384]{0:T(1024)S(1)} %bitcast.177, f32[32]{0:T(128)S(1)} %dynamic_slice.11, f32[16384]{0:T(1024)S(1)} %bitcast.178, f32[16384]{0:T(1024)S(1)} %bitcast.179, f32[32]{0:T(128)S(1)} %dynamic_slice.10, f32[16384]{0:T(1024)S(1)} %bitcast.116, ...), kind=kLoop, calls=%fused_computation.17 | loop fusion | flops 7339999 | bytes 4653476 | tf_op jit(solution)/shard_map/reduce_sum | solution.py:84
  143.4 39.5 %psum.7 = f32[]{:T(128)} all-reduce(f32[]{:T(128)} %get-tuple-element.3), channel_id=1, replica_groups=mesh['trade'=4,'node'=8] {'trade','node'}, use_global_device_ids=true, to_apply=%region_19.20 | all-reduce | flops 1 | bytes 8 | tf_op jit(solution)/shard_map/psum | solution.py:84
  (37 shorter events, 4.0 us)
Async XLA Ops:
  7.2 69.7 %all-gather.3.cloned.1.call-start = ((), (), s32[]{:S(2)}) async-start(), calls=%async_computation.1 | async-start | bytes 7077888 | tf_op jit(solution)/shard_map/all_gather | solution.py:82
  12.5 0.9 copy-start.1
  13.4 5.4 %copy-start.2 = (s32[256]{0:T(256)S(1)}, s32[256]{0:T(256)}, u32[]{:S(2)}) copy-start(s32[256]{0:T(256)} %param.20) | copy-start | bytes 3076
  13.4 5.5 %copy-start.3 = (s32[256]{0:T(256)S(1)}, s32[256]{0:T(256)}, u32[]{:S(2)}) copy-start(s32[256]{0:T(256)} %param.19) | copy-start | bytes 3076
  13.5 5.5 %copy-start.5 = (f32[64]{0:T(128)S(1)}, f32[64]{0:T(128)}, u32[]{:S(2)}) copy-start(f32[64]{0:T(128)} %param.21) | copy-start | bytes 772
  13.5 5.6 %copy-start.4 = (s32[256,4]{0,1:T(4,128)S(1)}, s32[256,4]{0,1:T(4,128)}, u32[]{:S(2)}) copy-start(s32[256,4]{0,1:T(4,128)} %param.18) | copy-start | bytes 12292
  13.5 40.3 %all-to-all-start = ((f32[8,32,2048]{2,1,0:T(8,128)}), f32[8,32,2048]{2,1,0:T(8,128)S(1)}, u32[]{:S(2)}, u32[]{:S(2)}) async-start(f32[8,32,2048]{2,1,0:T(8,128)} %bitcast.110), calls=%async_computation | async-start | bytes 4194304 | tf_op jit(solution)/shard_map/all_to_all | solution.py:40
  53.8 1.3 copy-start
Sparse Core Ops, SparseCore 0:
  13.6 63.2 all-gather.2
